TPU v7x, 128 devices: a whole 4x4x4 slice. The times are simulated.
128 devices in a mesh: freq: 16 (over z, x_lo, core), mode: 8 (over x_hi, y).
Axes of the slice: x: 4 (x_hi: 2, x_lo: 2; x = x_hi * 2 + x_lo), y: 4, z: 4, core: 2. Of those that a mesh axis runs over, the one named last changes fastest.
Arguments:
- sources: bfloat16 [32, 512, 2, 4096], P(None, None, None, ('freq', 'mode')), may hold values from -6 to 6
- mapping: bfloat16 [32, 2, 2048, 4096], P('freq', None, 'mode'), may hold values from -0.0625 to 0.0625
Outputs:
- pressure: bfloat16 [32, 512, 2, 2048], P(None, 'freq', None, 'mode')
All inputs are finite; a program needn't handle non-finite values.
Results may differ from a plain program's by a relative error of at most 0.0006.
Values may be sent and summed in bfloat16 or wider, within the bound.
No kernel may reach another device: no remote copies, remote signals or barrier semaphores. Data moves between devices by JAX's collectives and lax.ppermute only.
A program may use at most 128 MiB of HBM per device.

v0:
```python
import jax
import jax.numpy as jnp
from jax import lax
from jax.sharding import Mesh
from jax.sharding import PartitionSpec as P

FREQ = ("freq_0", "freq_1", "freq_2")
MODE = ("mode_0", "mode_1")
FREQ_MODE = ("freq_0", "freq_1", "freq_2", "mode_0", "mode_1")


def over_axes(x, axes):
    for axis in axes:
        x = lax.psum(x, axis)
    return x


def body(sources, mapping):
    freq_count = lax.axis_size(FREQ)
    mode_count = lax.axis_size(MODE)
    bin_count = mapping.shape[0]
    slice_width = sources.shape[3]
    regrouped = lax.all_to_all(sources, FREQ, split_axis=0, concat_axis=3, tiled=True)
    snapshots = regrouped.shape[1]
    blocked = regrouped.reshape(bin_count, snapshots, 2, 1, freq_count, slice_width)
    gathered = lax.all_gather(blocked, MODE, axis=3, tiled=True)
    complete = jnp.swapaxes(gathered, 3, 4).reshape(bin_count, snapshots, 2, -1)
    real_part = jnp.einsum(
        "bsm,bom->bso", complete[:, :, 0], mapping[:, 0], preferred_element_type=jnp.float32
    ) - jnp.einsum(
        "bsm,bom->bso", complete[:, :, 1], mapping[:, 1], preferred_element_type=jnp.float32
    )
    imag_part = jnp.einsum(
        "bsm,bom->bso", complete[:, :, 1], mapping[:, 0], preferred_element_type=jnp.float32
    ) + jnp.einsum(
        "bsm,bom->bso", complete[:, :, 0], mapping[:, 1], preferred_element_type=jnp.float32
    )
    field = jnp.stack([real_part, imag_part], axis=2)
    bins_total = bin_count * freq_count
    first_bin = lax.axis_index(FREQ) * bin_count
    bin_index = (first_bin + jnp.arange(bin_count, dtype=jnp.int32)).astype(jnp.float32)
    weights = ((bin_index + 1.0) / bins_total) ** 2
    local_energy = jnp.sum(weights[:, None, None, None] * field * field)
    energy = over_axes(local_energy, FREQ_MODE)
    energy = energy / (field.shape[1] * field.shape[3] * mode_count)
    factor = jnp.sqrt(bins_total / (energy + 1e-06))
    result = lax.all_to_all(
        (field * factor).astype(jnp.bfloat16), FREQ, split_axis=1, concat_axis=0, tiled=True
    )
    return result


def solution(mesh):
    torus = Mesh(
        mesh.devices.reshape(4, 2, 2, 2, 4), ("freq_0", "freq_1", "freq_2", "mode_0", "mode_1")
    )
    return jax.shard_map(
        body,
        mesh=torus,
        in_specs=(P(None, None, None, FREQ_MODE), P(FREQ, None, MODE, None)),
        out_specs=P(None, FREQ, None, MODE),
        check_vma=False,
    )
```

profile of v0, /device:TPU:1, one launch (start us, length us, event | category | flops | bytes accessed | tf_op | source)
XLA Modules:
  0.0 335.5 jit_solution(6700115910363452215)
XLA Ops:
  6.5 0.0 all-gather.3.cloned.1.call-start
  6.5 34.4 %all_to_all.33 = bf16[32,512,2,32]{1,3,2,0:T(8,128)(2,1)} all-to-all(bf16[32,512,2,32]{1,3,2,0:T(8,128)(2,1)} %param.2), channel_id=1, replica_groups=mesh['freq_0'=4,'freq_1'=2,'freq_2'=2,'mode_0'=2,'mode_1'=4] {'freq_0','..., dimensions={0} | all-to-all | bytes 4194304 | tf_op jit(solution)/shard_map/all_to_all | solution.py:23
  40.9 0.0 all-gather.3.cloned.1.call-update
  40.9 181.0 %all-gather.3.cloned.1.call-done = bf16[2,512,2,128,32]{1,4,2,0,3:T(8,128)(2,1)} async-done(((bf16[2,512,2,16,32]{1,4,2,0,3:T(8,128)(2,1)}), bf16[2,512,2,128,32]{1,4,2,0,3:T(8,128)(2,1)}) %all-gather.3.cloned.1.call-update) | async-done | bytes 16777232 | tf_op jit(solution)/shard_map/all_gather | solution.py:26
  222.0 14.2 %copy.20 = bf16[2,512,2,16,8,32]{1,5,4,3,2,0:T(8,128)(2,1)} copy(bf16[2,512,2,16,8,32]{1,5,2,0,3,4:T(8,128)(2,1)} %bitcast.57) | data formatting | bytes 33554432 | tf_op jit(solution)/shard_map/transpose | solution.py:27
  236.1 7.9 %fusion.1 = f32[2,512,256]{2,1,0:T(8,128)S(1)} fusion(bf16[2,512,2,4096]{1,3,2,0:T(8,128)(2,1)} %bitcast.58, bf16[2,2,256,4096]{3,2,1,0:T(8,128)(2,1)} %param.3), kind=kOutput, calls=%fused_computation.3 | convolution fusion | flops 2147483648 | bytes 13631488 | tf_op jit(solution)/shard_map/bsm,bom->bso/dot_general | solution.py:28
  244.0 7.9 %fusion = f32[2,512,256]{2,1,0:T(8,128)S(1)} fusion(bf16[2,512,2,4096]{1,3,2,0:T(8,128)(2,1)} %bitcast.59, bf16[2,2,256,4096]{3,2,1,0:T(8,128)(2,1)} %param.3), kind=kOutput, calls=%fused_computation.2 | convolution fusion | flops 2147483648 | bytes 13631488 | tf_op jit(solution)/shard_map/bsm,bom->bso/dot_general | solution.py:35
  252.0 7.9 %fusion.16 = f32[2,512,1,256]{3,1,0,2:T(8,128)S(1)} fusion(f32[2,512,256]{2,1,0:T(8,128)S(1)} %fusion.1, bf16[2,2,256,4096]{3,2,1,0:T(8,128)(2,1)} %param.3, bf16[2,512,2,4096]{1,3,2,0:T(8,128)(2,1)} %bitcast.60), kind=kOutput, calls=%fused_computation.19 | convolution fusion | flops 2147745792 | bytes 14680064 | tf_op jit(solution)/shard_map/bsm,bom->bso/dot_general | solution.py:30
  259.9 8.1 %fusion.22 = f32[2,512,1,256]{3,1,0,2:T(8,128)S(1)} fusion(f32[2,512,256]{2,1,0:T(8,128)S(1)} %fusion, bf16[2,2,256,4096]{3,2,1,0:T(8,128)(2,1)} %param.3, bf16[2,512,2,4096]{1,3,2,0:T(8,128)(2,1)} %bitcast.61), kind=kOutput, calls=%fused_computation.21 | convolution fusion | flops 2147745792 | bytes 14680064 | tf_op jit(solution)/shard_map/bsm,bom->bso/dot_general | solution.py:33
  268.0 1.2 fusion.12
  269.3 9.3 %psum.35 = f32[]{:T(128)} all-reduce(f32[]{:T(128)} %fusion.12), channel_id=1, replica_groups=mesh['freq_0'=4,'freq_1'=2,'freq_2'=2,'mode_0'=2,'mode_1'=4] {'freq_0'}, use_global_device_ids=true, to_apply=%region_1.0 | all-reduce | flops 1 | bytes 8 | tf_op jit(solution)/shard_map/psum | solution.py:14
  278.5 4.4 %psum.36 = f32[]{:T(128)} all-reduce(f32[]{:T(128)} %psum.35), channel_id=1, replica_groups=mesh['freq_0'=4,'freq_1'=2,'freq_2'=2,'mode_0'=2,'mode_1'=4] {'freq_1'}, use_global_device_ids=true, to_apply=%region_2.0 | all-reduce | flops 1 | bytes 8 | tf_op jit(solution)/shard_map/psum | solution.py:14
  282.9 7.3 %psum.37 = f32[]{:T(128)} all-reduce(f32[]{:T(128)} %psum.36), channel_id=1, replica_groups=mesh['freq_0'=4,'freq_1'=2,'freq_2'=2,'mode_0'=2,'mode_1'=4] {'freq_2'}, use_global_device_ids=true, to_apply=%region_3.0 | all-reduce | flops 1 | bytes 8 | tf_op jit(solution)/shard_map/psum | solution.py:14
  290.2 5.9 %psum.38 = f32[]{:T(128)} all-reduce(f32[]{:T(128)} %psum.37), channel_id=1, replica_groups=mesh['freq_0'=4,'freq_1'=2,'freq_2'=2,'mode_0'=2,'mode_1'=4] {'mode_0'}, use_global_device_ids=true, to_apply=%region_4.0 | all-reduce | flops 1 | bytes 8 | tf_op jit(solution)/shard_map/psum | solution.py:14
  296.1 7.1 %psum.39 = f32[]{:T(128)} all-reduce(f32[]{:T(128)} %psum.38), channel_id=1, replica_groups=mesh['freq_0'=4,'freq_1'=2,'freq_2'=2,'mode_0'=2,'mode_1'=4] {'mode_1'}, use_global_device_ids=true, to_apply=%region_5.0 | all-reduce | flops 1 | bytes 8 | tf_op jit(solution)/shard_map/psum | solution.py:14
  304.0 0.2 multiply_convert_fusion
  304.2 1.1 copy.25
  305.3 21.3 %all_to_all.34 = bf16[2,512,2,256]{3,0,2,1:T(2,128)(2,1)S(1)} all-to-all(bf16[2,512,2,256]{3,0,2,1:T(2,128)(2,1)S(1)} %copy.25), channel_id=1, replica_groups=mesh['freq_0'=4,'freq_1'=2,'freq_2'=2,'mode_0'=2,'mode_1'=4] {'freq_0','..., dimensions={1} | all-to-all | bytes 2097152 | tf_op jit(solution)/shard_map/all_to_all | solution.py:47
  326.6 2.1 copy.26
  (1 shorter events, 0.0 us)
Async XLA Ops:
  6.5 215.4 %all-gather.3.cloned.1.call-start = ((), (), s32[]{:S(2)}) async-start(), calls=%async_computation.2 | async-start | bytes 18874368 | tf_op jit(solution)/shard_map/all_gather | solution.py:26
Sparse Core Ops, SparseCore 0:
  41.0 180.8 all-gather.2
where the time goes:
time: 336 us
  waiting for transfers between devices  181 us (54%)
  blocking collectives  89.7 us (27%)
  matrix products  31.9 us (9%)
  local copies, waits for them, and re-layouts  17.3 us (5%)
  between operations  14.2 us (4%)
    all_gather x1, waiting for transfers between devices, body(): gathered = lax.all_gather(blocked, MODE, axis=3, tiled=True)  181 us
    all_to_all x1, blocking collectives, body(): lax.all_to_all(sources, FREQ, split_axis=0, concat_axis=3, tiled=True)  34.4 us
    psum x5, blocking collectives, over_axes(): x = lax.psum(x, axis)  34 us
    all_to_all x1, blocking collectives, body(): lax.all_to_all((field * factor).astype(jnp.bfloat16), FREQ, split_axis=1,...  21.3 us
    transpose x1, local copies, waits for them, and re-layouts, body(): complete = jnp.swapaxes(gathered, 3, 4).reshape(bin_count, snapshots, 2, -1)  14.2 us
    dot_general x1, matrix products, body(): jnp.einsum('bsm,bom->bso', complete[:, :, 1], mapping[:, 0], preferred_el...  8.11 us
    dot_general x1, matrix products, body(): jnp.einsum('bsm,bom->bso', complete[:, :, 1], mapping[:, 1], preferred_el...  7.93 us
    dot_general x1, matrix products, body(): jnp.einsum('bsm,bom->bso', complete[:, :, 0], mapping[:, 1], preferred_el...  7.93 us
  transfers between devices with their start and end apart: 1, of which 1 were waited for; matrix products, arithmetic and copies ran while one was open for 0% of the time, Pallas kernels for 0%

commit v1 on v0

v1 whole, which is shorter than its diff:
```python
import jax
import jax.numpy as jnp
from jax import lax
from jax.experimental import pallas as pl
from jax.experimental.pallas import tpu as pltpu
from jax.sharding import Mesh
from jax.sharding import PartitionSpec as P


FREQ = ("freq_0", "freq_1", "freq_2")
MODE = ("mode_0", "mode_1")
AXES = ("freq_0", "freq_1", "freq_2", "mode_0", "mode_1")
BF16 = jnp.bfloat16
F32 = jnp.float32


def linear(z, x, c, y):
    return (((z % 4 * 2 + x % 2) * 2 + c % 2) * 2 + x % 4 // 2) * 4 + y % 4


def hop(value, target):
    pairs = [
        (linear(z, x, c, y), linear(*target(z, x, c, y)))
        for z in range(4)
        for x in range(4)
        for c in range(2)
        for y in range(4)
    ]
    return lax.ppermute(value, AXES, pairs)


def vmem_call(kernel, out_shapes, where, *arrays):
    outs = [jax.ShapeDtypeStruct(s, d) for s, d in out_shapes]
    moved = sum(a.size * a.dtype.itemsize for a in arrays) * 2
    return pl.pallas_call(
        kernel,
        out_shape=outs,
        grid_spec=pltpu.PrefetchScalarGridSpec(
            num_scalar_prefetch=1,
            grid=(1,),
            in_specs=[whole(a.shape) for a in arrays],
            out_specs=[whole(s) for s, _ in out_shapes],
        ),
        cost_estimate=pl.CostEstimate(flops=moved, bytes_accessed=moved, transcendentals=0),
    )(where, *arrays)


def whole(shape):
    return pl.BlockSpec(shape, lambda g, w: (0,) * len(shape))


def pack_early_kernel(where, t_ref, *outs):
    z, xl, c, y = where[0], where[1], where[2], where[4]
    for peer in range(8):
        zt, ct = (z + peer % 4) % 4, c ^ (peer // 4)
        for i in range(2):
            lanes = pl.ds(pl.multiple_of((zt + 1 + i) % 4 * 128, 128), 128)
            for brel in range(2):
                for xrel in range(2):
                    outs[peer][i, brel, xrel] = t_ref[
                        zt, xl ^ xrel, ct, (y % 2) ^ brel, :, :, lanes
                    ]


def pack_late_kernel(where, t_ref, out):
    xl, y = where[1], where[4]
    for peer in range(8):
        zt, ct = peer // 2, peer % 2
        for i in range(2):
            k = (zt + 3 + i) % 4
            for brel in range(2):
                for xrel in range(2):
                    out[peer, i, brel, xrel] = t_ref[
                        zt, xl ^ xrel, ct, (y % 2) ^ brel, :, :, k * 128 : k * 128 + 128
                    ]


def join_early_kernel(where, *refs):
    pieces, outs = refs[:8], refs[8:]
    z, c = where[0], where[2]
    for peer in range(8):
        s = (z + 4 - peer % 4) % 4 * 2 + (c ^ (peer // 4))
        for part in range(2):
            for xrel in range(2):
                outs[part * 2][xrel, s] = pieces[peer][part, 0, xrel]
                outs[part * 2 + 1][xrel, s] = pieces[peer][part, 1, xrel]


def join_late_kernel(where, pieces, *outs):
    for part in range(2):
        for s in range(8):
            for xrel in range(2):
                outs[part * 2][xrel, s] = pieces[s, part, 0, xrel]
                outs[part * 2 + 1][xrel, s] = pieces[s, part, 1, xrel]


def join_x_kernel(where, *refs):
    pieces, (same, other) = refs[:4], refs[4:]
    for s in range(4):
        same[s] = pieces[s][0]
        other[s] = pieces[s][1]


ROWS = 128


def order_rows(where, pieces, full):
    xl, xh, y = where[1], where[3], where[4]
    x = xh * 2 + xl
    for dx, piece in zip((0, 2, 3, 1), pieces):
        xs = (x + dx) % 4
        for yi, dy in enumerate((0, 2, 3, 1)):
            ys = (y + dy) % 4
            for s in range(8):
                row = s // 2 * 1024 + (xs % 2) * 512 + s % 2 * 256 + (xs // 2) * 128 + ys * 32
                rows = pl.ds(pl.multiple_of(row, 32), 32)
                full[rows, 0:128] = piece[yi, s, 0]
                full[rows, 128:256] = piece[yi, s, 1]


def field_kernel(closing, where, *refs):
    pieces, refs, full = refs[:4], refs[4:-1], refs[-1]
    if closing:
        before, running, refs = refs[5:8], refs[-1], refs[:5] + refs[8:-1]
    own, near_r0, near_i0, near_r1, near_i1, out, energy = refs
    if not closing:
        running = energy

    @pl.when(pl.program_id(0) == 0)
    def _():
        order_rows(where, pieces, full)
        if closing:
            running[...] = before[0][...] + before[1][...] + before[2][...]
        else:
            running[...] = jnp.zeros_like(running)

    total = jnp.zeros((8, 128), F32)
    spectra = full[...]

    def times(*lefts):
        width = 4096 // len(lefts)
        parts = [
            jnp.dot(left, spectra[n * width : n * width + width], preferred_element_type=F32)
            for n, left in enumerate(lefts)
        ]
        return sum(parts[1:], parts[0])

    for o, (with_r, with_i) in enumerate(
        (
            (times(own[0, 0]), times(own[0, 1])),
            (times(near_r0[...], near_r1[...]), times(near_i0[...], near_i1[...])),
        )
    ):
        real = with_r[:, :128] - with_i[:, 128:]
        imag = with_r[:, 128:] + with_i[:, :128]
        square = real * real + imag * imag
        total = total + jnp.sum(square.reshape(ROWS // 8, 8, 128), axis=0)
        for part, value in enumerate((real, imag)):
            value = value.T
            for q in range(4):
                out[o, q, part] = value[q * 32 : q * 32 + 32]
    running[...] += total
    if closing:
        number = ((where[0] * 2 + where[1]) * 2 + where[2]) * 2 + where[4] % 2 + 1
        weight = (number.astype(F32) / 32) ** 2
        line = jnp.sum(running[...], axis=0, keepdims=True) * weight
        energy[...] = jnp.broadcast_to(line, energy.shape)


def field_call(where, spectra, mapping, near, before=()):
    closing = len(before) > 0
    lines = (128, 128) if closing else (8, 128)
    shape = (2, 4, 2, 32, 256)
    scratch = [pltpu.VMEM((8, 128), F32)] if closing else []
    return pl.pallas_call(
        lambda *r: field_kernel(closing, *r),
        out_shape=[jax.ShapeDtypeStruct(s, F32) for s in (shape, lines)],
        grid_spec=pltpu.PrefetchScalarGridSpec(
            num_scalar_prefetch=1,
            grid=(256 // ROWS,),
            in_specs=[whole(a.shape) for a in spectra]
            + [pl.BlockSpec((1, 2, ROWS, 4096), lambda g, w: (w[4] % 2, 0, g, 0))]
            + [pl.BlockSpec((ROWS, 2048), lambda g, w: (g, 0))] * 4
            + [whole((8, 128))] * len(before),
            out_specs=[
                pl.BlockSpec((2, 4, 2, 32, ROWS), lambda g, w: (0, 0, 0, 0, g)),
                pl.BlockSpec(lines, lambda g, w: (0, 0)),
            ],
            scratch_shapes=scratch + [pltpu.VMEM((4096, 256), BF16)],
        ),
        cost_estimate=pl.CostEstimate(flops=2 * 1024 * 4096 * 256, bytes_accessed=11 << 20, transcendentals=0),
        compiler_params=pltpu.CompilerParams(vmem_limit_bytes=48 << 20),
    )(where, *spectra, mapping, *near, *before)


def take_kernel(where, rows_ref, out):
    out[...] = rows_ref[0, 0]


def take_mapping(where, mapping, part, half):
    return pl.pallas_call(
        take_kernel,
        out_shape=jax.ShapeDtypeStruct((256, 2048), BF16),
        grid_spec=pltpu.PrefetchScalarGridSpec(
            num_scalar_prefetch=1,
            grid=(2,),
            in_specs=[pl.BlockSpec((1, 1, 128, 2048), lambda g, w: (1 - w[4] % 2, part, g, half))],
            out_specs=pl.BlockSpec((128, 2048), lambda g, w: (g, 0)),
        ),
        cost_estimate=pl.CostEstimate(flops=2 << 20, bytes_accessed=2 << 20, transcendentals=0),
    )(where, mapping)


def scale_kernel(where, shared, *refs):
    fields, outs = refs[:4], refs[4:]
    energy = jnp.sum(shared[...]) / (512 * 2048)
    factor = jnp.sqrt(32 / (energy + 1e-06))
    for d in range(4):
        q = (where[1] * 2 + where[2]) ^ d
        for o in range(2):
            for i in range(4):
                outs[o * 4 + d][i] = (fields[i][o, q] * factor).astype(BF16)


def last_kernel(where, *refs):
    parts, out = refs[:8], refs[8]
    z, xl, c, y = where[0], where[1], where[2], where[4]
    for o in range(2):
        for d in range(4):
            for i in range(4):
                zs = (z + 3 - i) % 4
                row = zs * 8 + (d ^ (xl * 2 + c)) * 2 + (y + o) % 2
                out[row, :, 0, :] = parts[o * 4 + d][i, 0]
                out[row, :, 1, :] = parts[o * 4 + d][i, 1]


def return_hop(value, n):
    o, xrel, crel = n // 4, n // 2 % 2, n % 2
    return hop(value, lambda z, x, c, y: (z, x ^ xrel, c ^ crel, y + (o if c == 0 else -o)))


def return_all(parts):
    landed = {n: return_hop(parts[n], n) for n in (2, 3, 6, 7, 4, 5, 1)}
    return [parts[0]] + [landed[n] for n in range(1, 8)]


def steps(sources, mapping):
    where = jnp.stack([lax.axis_index(a) for a in AXES]).astype(jnp.int32)
    table = jnp.transpose(sources, (0, 2, 3, 1)).reshape(4, 2, 2, 2, 2, 32, 512)
    block = (2, 2, 2, 32, 128)
    blocks = vmem_call(pack_early_kernel, [((2,) + block, BF16)] * 8, where, table)
    late = vmem_call(pack_late_kernel, [((8, 2) + block, BF16)], where, table)[0]
    early = [blocks[0]]
    for n in range(1, 8):
        crel, dz = n // 4, n % 4
        early.append(hop(blocks[n], lambda z, x, c, y: (z + dz, x, c + crel, y)))
    late = lax.all_to_all(
        late, ("freq_0", "freq_2"), split_axis=0, concat_axis=0, tiled=True
    )

    near = []
    for n in range(4):
        rows = take_mapping(where, mapping, n % 2, n // 2)
        near.append(hop(rows, lambda z, x, c, y: (z, x, c, y + (1 if c else 3))))

    yshape = (2, 8, 2, 32, 128)
    xshape = (4, 8, 2, 32, 128)
    joined = vmem_call(join_early_kernel, [(yshape, BF16)] * 4, where, *early)
    joined += vmem_call(join_late_kernel, [(yshape, BF16)] * 4, where, late)

    fields, energies = [], []
    for i in range(4):
        same, other = joined[2 * i], joined[2 * i + 1]
        y2 = hop(same, lambda z, x, c, y: (z, x, c, y + 2))
        yp = hop(other, lambda z, x, c, y: (z, x, c, y + 1))
        ym = hop(other, lambda z, x, c, y: (z, x, c, y + 3))
        same, other = vmem_call(join_x_kernel, [(xshape, BF16)] * 2, where, same, y2, yp, ym)
        x2 = hop(same, lambda z, x, c, y: (z, x + 2, c, y))
        xp = hop(other, lambda z, x, c, y: (z, x + 1, c, y))
        xm = hop(other, lambda z, x, c, y: (z, x + 3, c, y))
        spectra = (same, x2, xp, xm)
        field, energy = field_call(where, spectra, mapping, near, energies if i == 3 else ())
        energies.append(energy)
        if i < 3:
            field = hop(field, lambda z, x, c, y: (z + 1 + i, x, c, y))
        fields.append(field)

    shared = lax.all_to_all(energy, AXES, split_axis=0, concat_axis=0, tiled=True)

    parts = vmem_call(
        scale_kernel, [((4, 2, 32, 256), BF16)] * 8, where, shared, *fields
    )
    landed = return_all(parts)
    return vmem_call(last_kernel, [((32, 32, 2, 256), BF16)], where, *landed)[0]


def solution(mesh):
    torus = Mesh(mesh.devices.reshape(4, 2, 2, 2, 4), AXES)
    return jax.shard_map(
        steps,
        mesh=torus,
        in_specs=(P(None, None, None, AXES), P(FREQ, None, MODE, None)),
        out_specs=P(None, FREQ, None, MODE),
        check_vma=False,
    )
```

time: 336 us -> 241 us (0.72)
  waiting for transfers between devices: 181 us -> 88.7 us
  blocking collectives: 89.7 us -> 0 us
  starting transfers between devices: 0.01 us -> 74 us
  Pallas kernels: 0 us -> 68.2 us
  matrix products: 31.9 us -> 0 us
  between operations: 14.2 us -> 0.26 us
  local copies, waits for them, and re-layouts: 17.3 us -> 9.45 us
    all_gather x1 -> x0, waiting for transfers between devices: 181 us -> none  [body(): gathered = lax.all_gather(blocked, MODE, axis=3, tiled=True)]
    ppermute x0 -> x45, waiting for transfers between devices: none -> 78.9 us  [hop(): return lax.ppermute(value, AXES, pairs)]
    pallas_call x0 -> x18, Pallas kernels: none -> 68.2 us  [the longest x10 31.7 us: vmem_call(): pl.pallas_call(kernel, out_shape=outs, grid_spec=pltpu.PrefetchScalarGrid...]
    ppermute x0 -> x45, starting transfers between devices: none -> 62.5 us  [hop(): return lax.ppermute(value, AXES, pairs)]
    all_to_all x2 -> x0, blocking collectives: 55.7 us -> none  [the longest x1 34.4 us: body(): lax.all_to_all(sources, FREQ, split_axis=0, concat_axis=3, tiled=True)]
    psum x5 -> x0, blocking collectives: 34 us -> none  [over_axes(): x = lax.psum(x, axis)]
    dot_general x4 -> x0, matrix products: 31.9 us -> none  [the longest x1 8.11 us: body(): jnp.einsum('bsm,bom->bso', complete[:, :, 1], mapping[:, 0], preferred_el...]
    transpose x1 -> x0, local copies, waits for them, and re-layouts: 14.2 us -> none  [body(): complete = jnp.swapaxes(gathered, 3, 4).reshape(bin_count, snapshots, 2, -1)]
  transfers between devices with their start and end apart: 1 -> 47, of which waited for: 1 -> 18; matrix products, arithmetic and copies ran while one was open for 0% -> 0% of each run, Pallas kernels for 0% -> 23%
where the time goes in v1:
time: 241 us
  waiting for transfers between devices  88.7 us (37%)
  starting transfers between devices  74 us (31%)
  Pallas kernels  68.2 us (28%)
  local copies, waits for them, and re-layouts  9.45 us (4%)
    ppermute x45, waiting for transfers between devices, hop(): return lax.ppermute(value, AXES, pairs)  78.9 us
    ppermute x45, starting transfers between devices, hop(): return lax.ppermute(value, AXES, pairs)  62.5 us
    pallas_call x10, Pallas kernels, vmem_call(): pl.pallas_call(kernel, out_shape=outs, grid_spec=pltpu.PrefetchScalarGrid...  31.7 us
    pallas_call x4, Pallas kernels, field_call(): pl.pallas_call(lambda *r: field_kernel(closing, *r), out_shape=[jax.Shape...  25.5 us
    pallas_call x4, Pallas kernels, take_mapping(): pl.pallas_call(take_kernel, out_shape=jax.ShapeDtypeStruct((256, 2048), B...  10.9 us
    all_to_all x1, waiting for transfers between devices, steps(): lax.all_to_all(energy, AXES, split_axis=0, concat_axis=0, tiled=True)  9.81 us
    unnamed x64, local copies, waits for them, and re-layouts  8.82 us
    all_to_all x1, starting transfers between devices, steps(): lax.all_to_all(late, ('freq_0', 'freq_2'), split_axis=0, concat_axis=0, t...  6.12 us
  transfers between devices with their start and end apart: 47, of which 18 were waited for; matrix products, arithmetic and copies ran while one was open for 0% of the time, Pallas kernels for 23%

profile of v1, /device:TPU:1, one launch (start us, length us, event | category | flops | bytes accessed | tf_op | source)
XLA Modules:
  0.0 240.6 jit_solution(5991252006511675519)
XLA Ops:
  0.6 3.4 %shard_map.35 = (bf16[2,2,2,2,32,128]{5,4,3,2,1,0:T(8,128)(2,1)}, bf16[2,2,2,2,32,128]{5,4,3,2,1,0:T(8,128)(2,1)}, bf16[2,2,2,2,32,128]{5,4,3,2,1,0:T(8,128)(2,1...) custom-call(s32[5]{0:T(128)} %stack.23.where.r_0_, ...), custom_call_target="tpu_custom_call" | custom-call | flops 4194304 | bytes 4194304 | tf_op jit(solution)/shard_map/pallas_call | solution.py:35
  4.0 2.5 %collective-permute-start.10 = (bf16[2,2,2,2,32,128]{5,4,3,2,1,0:T(8,128)(2,1)}, bf16[2,2,2,2,32,128]{5,4,3,2,1,0:T(8,128)(2,1)S(1)}, u32[]{:S(2)}, u32[]{:S(2)}) collective-permute-start(bf16[2,2,2,2,32,128]{5,4,3,2,1,0:T(8,128)(2,1)} %get-tuple-element.50), channel_id=1, source_target_pairs={{0,32},{1,33},{2,34},{3,35},{8,40},{9,41},{10,42},{11,43},{16,48},... | collective-permute-start | bytes 393224 | tf_op jit(solution)/shard_map/ppermute | solution.py:29
  6.5 3.3 %collective-permute-start.11 = (bf16[2,2,2,2,32,128]{5,4,3,2,1,0:T(8,128)(2,1)}, bf16[2,2,2,2,32,128]{5,4,3,2,1,0:T(8,128)(2,1)S(1)}, u32[]{:S(2)}, u32[]{:S(2)}) collective-permute-start(bf16[2,2,2,2,32,128]{5,4,3,2,1,0:T(8,128)(2,1)} %get-tuple-element.51), channel_id=1, source_target_pairs={{0,64},{1,65},{2,66},{3,67},{8,72},{9,73},{10,74},{11,75},{16,80},... | collective-permute-start | bytes 393224 | tf_op jit(solution)/shard_map/ppermute | solution.py:29
  10.5 1.5 collective-permute-start.13
  12.7 2.2 collective-permute-start.15
  14.9 0.9 collective-permute-done.11.refs_2_
  15.7 1.2 collective-permute-start.16
  16.9 5.4 %collective-permute-done.14.refs_5_ = bf16[2,2,2,2,32,128]{5,4,3,2,1,0:T(8,128)(2,1)S(1)} collective-permute-done((bf16[2,2,2,2,32,128]{5,4,3,2,1,0:T(8,128)(2,1)}, bf16[2,2,2,2,32,128]{5,4,3,2,1,0:T(8,128)(2,1)S(1)}, u32[]{:S(2)}, u32[]{:S(2)}) %collective-permute-start.14) | collective-permute-done | bytes 131104 | tf_op jit(solution)/shard_map/ppermute | solution.py:29
  23.1 3.0 %shard_map.36 = (bf16[2,8,2,32,128]{4,3,2,1,0:T(8,128)(2,1)}, bf16[2,8,2,32,128]{4,3,2,1,0:T(8,128)(2,1)}, bf16[2,8,2,32,128]{4,3,2,1,0:T(8,128)(2,1)}, bf16[2,8,2,32,128]{4,3,2,1,0:T(8,128)(2,1)}) custom-call(s32[5]{0:T(128)} %stack.23.where.r_0_, bf16[2,2,2,2,32,128]{5,4,3,2,1,0:T(8,128)(2,1)} %get-tuple-element.49.refs_0_, ...), custom_call_target="tpu_custom_call" | custom-call | flops 2097152 | bytes 2097152 | tf_op jit(solution)/shard_map/pallas_call | solution.py:35
  26.1 2.9 %collective-permute-start.23 = (bf16[2,8,2,32,128]{4,3,2,1,0:T(8,128)(2,1)}, bf16[2,8,2,32,128]{4,3,2,1,0:T(8,128)(2,1)S(1)}, u32[]{:S(2)}, u32[]{:S(2)}) collective-permute-start(bf16[2,8,2,32,128]{4,3,2,1,0:T(8,128)(2,1)} %get-tuple-element.62.refs_0_), channel_id=1, source_target_pairs={{0,2},{1,3},{2,0},{3,1},{8,10},{9,11},{10,8},{11,9},{16,18},{17,19... | collective-permute-start | bytes 786440 | tf_op jit(solution)/shard_map/ppermute | solution.py:29
  29.4 2.3 collective-permute-start.25
  31.7 3.3 %collective-permute-done.23.refs_1_ = bf16[2,8,2,32,128]{4,3,2,1,0:T(8,128)(2,1)S(1)} collective-permute-done((bf16[2,8,2,32,128]{4,3,2,1,0:T(8,128)(2,1)}, bf16[2,8,2,32,128]{4,3,2,1,0:T(8,128)(2,1)S(1)}, u32[]{:S(2)}, u32[]{:S(2)}) %collective-permute-start.23) | collective-permute-done | bytes 262176 | tf_op jit(solution)/shard_map/ppermute | solution.py:29
  35.0 7.8 %collective-permute-done.24.refs_2_ = bf16[2,8,2,32,128]{4,3,2,1,0:T(8,128)(2,1)S(1)} collective-permute-done((bf16[2,8,2,32,128]{4,3,2,1,0:T(8,128)(2,1)}, bf16[2,8,2,32,128]{4,3,2,1,0:T(8,128)(2,1)S(1)}, u32[]{:S(2)}, u32[]{:S(2)}) %collective-permute-start.24) | collective-permute-done | bytes 262176 | tf_op jit(solution)/shard_map/ppermute | solution.py:29
  44.2 2.9 %shard_map.39 = (bf16[4,8,2,32,128]{4,3,2,1,0:T(8,128)(2,1)}, bf16[4,8,2,32,128]{4,3,2,1,0:T(8,128)(2,1)}) custom-call(s32[5]{0:T(128)} %stack.23.where.r_0_, bf16[2,8,2,32,128]{4,3,2,1,0:T(8,128)(2,1)} %get-tuple-element.62.refs_0_, bf16[2,8,2,32,128]{4,3,2,1,0:T(8,128)(2,1)} %copy-done.14, bf16[2,8,2,32,128]{4,3,2,1,0:T(8,128)(2,1)} %copy-done.15, ...), custom_call_target="tpu_custom_call" | custom-call | flops 2097152 | bytes 2097152 | tf_op jit(solution)/shard_map/pallas_call | solution.py:35
  47.1 2.7 %collective-permute-start.26 = (bf16[4,8,2,32,128]{4,3,2,1,0:T(8,128)(2,1)}, bf16[4,8,2,32,128]{4,3,2,1,0:T(8,128)(2,1)S(1)}, u32[]{:S(2)}, u32[]{:S(2)}) collective-permute-start(bf16[4,8,2,32,128]{4,3,2,1,0:T(8,128)(2,1)} %get-tuple-element.64.r_1_), channel_id=1, source_target_pairs={{0,4},{1,5},{2,6},{3,7},{8,12},{9,13},{10,14},{11,15},{16,20},{17,... | collective-permute-start | bytes 1572872 | tf_op jit(solution)/shard_map/ppermute | solution.py:29
  50.4 2.1 collective-permute-start.19
  52.9 2.4 collective-permute-start.28
  55.2 3.4 %shard_map.28 = bf16[8,2,2,2,2,32,128]{6,5,4,3,2,1,0:T(8,128)(2,1)} custom-call(s32[5]{0:T(128)} %stack.23.where.r_0_, bf16[4,2,2,2,2,32,512]{6,5,4,3,2,1,0:T(8,128)(2,1)} %bitcast.13), custom_call_target="tpu_custom_call" | custom-call | flops 4194304 | bytes 4194304 | tf_op jit(solution)/shard_map/pallas_call | solution.py:35
  58.6 6.1 %all-to-all-start = ((bf16[8,2,2,2,2,32,128]{6,5,4,3,2,1,0:T(8,128)(2,1)}), bf16[8,2,2,2,2,32,128]{6,5,4,3,2,1,0:T(8,128)(2,1)}, u32[]{:S(2)}, u32[]{:S(2)}) async-start(bf16[8,2,2,2,2,32,128]{6,5,4,3,2,1,0:T(8,128)(2,1)} %shard_map.28), calls=%async_computation | async-start | bytes 2097152 | tf_op jit(solution)/shard_map/all_to_all | solution.py:257
  64.7 2.7 %shard_map.31 = bf16[256,2048]{1,0:T(8,128)(2,1)} custom-call(s32[5]{0:T(128)} %stack.23.where.r_0_, bf16[2,2,256,4096]{3,2,1,0:T(8,128)(2,1)} %r_5_.7), custom_call_target="tpu_custom_call" | custom-call | flops 2097152 | bytes 2097152 | tf_op jit(solution)/shard_map/pallas_call | solution.py:201
  67.7 2.8 %shard_map.32 = bf16[256,2048]{1,0:T(8,128)(2,1)} custom-call(s32[5]{0:T(128)} %stack.23.where.r_0_, bf16[2,2,256,4096]{3,2,1,0:T(8,128)(2,1)} %r_5_.7), custom_call_target="tpu_custom_call" | custom-call | flops 2097152 | bytes 2097152 | tf_op jit(solution)/shard_map/pallas_call | solution.py:201
  70.5 3.0 %shard_map.37 = (bf16[4,8,2,32,128]{4,3,2,1,0:T(8,128)(2,1)}, bf16[4,8,2,32,128]{4,3,2,1,0:T(8,128)(2,1)}) custom-call(s32[5]{0:T(128)} %stack.23.where.r_0_, bf16[2,8,2,32,128]{4,3,2,1,0:T(8,128)(2,1)} %get-tuple-element.57.refs_0_, bf16[2,8,2,32,128]{4,3,2,1,0:T(8,128)(2,1)} %copy-done.11, bf16[2,8,2,32,128]{4,3,2,1,0:T(8,128)(2,1)} %collective-permute-done.18.refs_2_, ...), custom_call_target="tpu_custom_call" | custom-call | flops 2097152 | bytes 2097152 | tf_op jit(solution)/shard_map/pallas_call | solution.py:35
  73.5 2.7 %shard_map.33 = bf16[256,2048]{1,0:T(8,128)(2,1)} custom-call(s32[5]{0:T(128)} %stack.23.where.r_0_, bf16[2,2,256,4096]{3,2,1,0:T(8,128)(2,1)} %r_5_.7), custom_call_target="tpu_custom_call" | custom-call | flops 2097152 | bytes 2097152 | tf_op jit(solution)/shard_map/pallas_call | solution.py:201
  77.3 1.4 collective-permute-start.8
  78.8 2.7 %shard_map.34 = bf16[256,2048]{1,0:T(8,128)(2,1)} custom-call(s32[5]{0:T(128)} %stack.23.where.r_0_, bf16[2,2,256,4096]{3,2,1,0:T(8,128)(2,1)} %r_5_.7), custom_call_target="tpu_custom_call" | custom-call | flops 2097152 | bytes 2097152 | tf_op jit(solution)/shard_map/pallas_call | solution.py:201
  81.5 6.3 %collective-permute-done.20.r_2_ = bf16[4,8,2,32,128]{4,3,2,1,0:T(8,128)(2,1)} collective-permute-done((bf16[4,8,2,32,128]{4,3,2,1,0:T(8,128)(2,1)}, bf16[4,8,2,32,128]{4,3,2,1,0:T(8,128)(2,1)}, u32[]{:S(2)}, u32[]{:S(2)}) %collective-permute-start.20) | collective-permute-done | bytes 524320 | tf_op jit(solution)/shard_map/ppermute | solution.py:29
  87.8 1.1 collective-permute-start.9
  89.0 2.9 %shard_map.29 = (bf16[2,8,2,32,128]{4,3,2,1,0:T(8,128)(2,1)}, bf16[2,8,2,32,128]{4,3,2,1,0:T(8,128)(2,1)}, bf16[2,8,2,32,128]{4,3,2,1,0:T(8,128)(2,1)}, bf16[2,8,2,32,128]{4,3,2,1,0:T(8,128)(2,1)}) custom-call(s32[5]{0:T(128)} %stack.23.where.r_0_, bf16[8,2,2,2,2,32,128]{6,5,4,3,2,1,0:T(8,128)(2,1)} %all-to-all-done.pieces), custom_call_target="tpu_custom_call" | custom-call | flops 2097152 | bytes 2097152 | tf_op jit(solution)/shard_map/pallas_call | solution.py:35
  91.9 8.5 %collective-permute-done.21.r_3_ = bf16[4,8,2,32,128]{4,3,2,1,0:T(8,128)(2,1)} collective-permute-done((bf16[4,8,2,32,128]{4,3,2,1,0:T(8,128)(2,1)}, bf16[4,8,2,32,128]{4,3,2,1,0:T(8,128)(2,1)}, u32[]{:S(2)}, u32[]{:S(2)}) %collective-permute-start.21) | collective-permute-done | bytes 524320 | tf_op jit(solution)/shard_map/ppermute | solution.py:29
  100.4 3.7 %collective-permute-start.29 = (bf16[2,8,2,32,128]{4,3,2,1,0:T(8,128)(2,1)}, bf16[2,8,2,32,128]{4,3,2,1,0:T(8,128)(2,1)S(1)}, u32[]{:S(2)}, u32[]{:S(2)}) collective-permute-start(bf16[2,8,2,32,128]{4,3,2,1,0:T(8,128)(2,1)} %get-tuple-element.67.refs_0_), channel_id=1, source_target_pairs={{0,2},{1,3},{2,0},{3,1},{8,10},{9,11},{10,8},{11,9},{16,18},{17,19... | collective-permute-start | bytes 786440 | tf_op jit(solution)/shard_map/ppermute | solution.py:29
  104.1 2.7 %collective-permute-start.31 = (bf16[2,8,2,32,128]{4,3,2,1,0:T(8,128)(2,1)}, bf16[2,8,2,32,128]{4,3,2,1,0:T(8,128)(2,1)}, u32[]{:S(2)}, u32[]{:S(2)}) collective-permute-start(bf16[2,8,2,32,128]{4,3,2,1,0:T(8,128)(2,1)} %get-tuple-element.68), channel_id=1, source_target_pairs={{0,3},{1,0},{2,1},{3,2},{8,11},{9,8},{10,9},{11,10},{16,19},{17,16... | collective-permute-start | bytes 786440 | tf_op jit(solution)/shard_map/ppermute | solution.py:29
  106.8 20.1 %collective-permute-done.29.refs_1_ = bf16[2,8,2,32,128]{4,3,2,1,0:T(8,128)(2,1)S(1)} collective-permute-done((bf16[2,8,2,32,128]{4,3,2,1,0:T(8,128)(2,1)}, bf16[2,8,2,32,128]{4,3,2,1,0:T(8,128)(2,1)S(1)}, u32[]{:S(2)}, u32[]{:S(2)}) %collective-permute-start.29) | collective-permute-done | bytes 262176 | tf_op jit(solution)/shard_map/ppermute | solution.py:29
  127.6 1.2 collective-permute-start
  128.8 1.6 collective-permute-done.30.refs_2_
  130.4 2.7 %collective-permute-start.2 = (bf16[2,8,2,32,128]{4,3,2,1,0:T(8,128)(2,1)}, bf16[2,8,2,32,128]{4,3,2,1,0:T(8,128)(2,1)}, u32[]{:S(2)}, u32[]{:S(2)}) collective-permute-start(bf16[2,8,2,32,128]{4,3,2,1,0:T(8,128)(2,1)} %get-tuple-element.46), channel_id=1, source_target_pairs={{0,3},{1,0},{2,1},{3,2},{8,11},{9,8},{10,9},{11,10},{16,19},{17,16... | collective-permute-start | bytes 786440 | tf_op jit(solution)/shard_map/ppermute | solution.py:29
  133.1 2.9 %shard_map.41 = (bf16[4,8,2,32,128]{4,3,2,1,0:T(8,128)(2,1)}, bf16[4,8,2,32,128]{4,3,2,1,0:T(8,128)(2,1)}) custom-call(s32[5]{0:T(128)} %stack.23.where.r_0_, bf16[2,8,2,32,128]{4,3,2,1,0:T(8,128)(2,1)} %get-tuple-element.67.refs_0_, bf16[2,8,2,32,128]{4,3,2,1,0:T(8,128)(2,1)} %copy-done.13, bf16[2,8,2,32,128]{4,3,2,1,0:T(8,128)(2,1)} %collective-permute-done.30.refs_2_, ...), custom_call_target="tpu_custom_call" | custom-call | flops 2097152 | bytes 2097152 | tf_op jit(solution)/shard_map/pallas_call | solution.py:35
  136.0 0.9 collective-permute-start.32
  136.9 3.4 %collective-permute-done.1.refs_2_ = bf16[2,8,2,32,128]{4,3,2,1,0:T(8,128)(2,1)} collective-permute-done((bf16[2,8,2,32,128]{4,3,2,1,0:T(8,128)(2,1)}, bf16[2,8,2,32,128]{4,3,2,1,0:T(8,128)(2,1)}, u32[]{:S(2)}, u32[]{:S(2)}) %collective-permute-start.1) | collective-permute-done | bytes 262176 | tf_op jit(solution)/shard_map/ppermute | solution.py:29
  140.2 1.2 collective-permute-done.2.refs_3_
  141.5 1.5 collective-permute-start.34
  142.9 2.9 %shard_map.30 = (bf16[4,8,2,32,128]{4,3,2,1,0:T(8,128)(2,1)}, bf16[4,8,2,32,128]{4,3,2,1,0:T(8,128)(2,1)}) custom-call(s32[5]{0:T(128)} %stack.23.where.r_0_, bf16[2,8,2,32,128]{4,3,2,1,0:T(8,128)(2,1)} %get-tuple-element.45.refs_0_, bf16[2,8,2,32,128]{4,3,2,1,0:T(8,128)(2,1)} %copy-done.12, bf16[2,8,2,32,128]{4,3,2,1,0:T(8,128)(2,1)} %collective-permute-done.1.refs_2_, ...), custom_call_target="tpu_custom_call" | custom-call | flops 2097152 | bytes 2097152 | tf_op jit(solution)/shard_map/pallas_call | solution.py:35
  145.8 1.0 copy-done
  146.9 1.0 copy-done.2
  147.9 1.0 copy-done.4
  149.0 6.3 %shard_map.40 = (f32[2,4,2,32,256]{4,3,2,1,0:T(8,128)}, f32[8,128]{1,0:T(8,128)S(1)}) custom-call(s32[5]{0:T(128)S(1)} %copy-done.9, bf16[4,8,2,32,128]{4,3,2,1,0:T(8,128)(2,1)S(1)} %copy-done, bf16[4,8,2,32,128]{4,3,2,1,0:T(8,128)(2,1)S(1)} %copy-done.2, bf16[4,8,2,32,128]{4,3,2,1,0:T(8,128)(2,1)S(1)} %copy-done.4, ...), custom_call_target="tpu_custom_call" | custom-call | flops 2147483648 | bytes 11534336 | tf_op jit(solution)/shard_map/pallas_call | solution.py:175
  155.2 5.2 %collective-permute-start.4 = (bf16[4,8,2,32,128]{4,3,2,1,0:T(8,128)(2,1)S(1)}, bf16[4,8,2,32,128]{4,3,2,1,0:T(8,128)(2,1)S(1)}, u32[]{:S(2)}, u32[]{:S(2)}) collective-permute-start(bf16[4,8,2,32,128]{4,3,2,1,0:T(8,128)(2,1)S(1)} %copy-done.31), channel_id=1, source_target_pairs={{0,16},{1,17},{2,18},{3,19},{8,24},{9,25},{10,26},{11,27},{16,4},{... | collective-permute-start | bytes 1572872 | tf_op jit(solution)/shard_map/ppermute | solution.py:29
  160.4 3.3 %collective-permute-start.5 = (bf16[4,8,2,32,128]{4,3,2,1,0:T(8,128)(2,1)S(1)}, bf16[4,8,2,32,128]{4,3,2,1,0:T(8,128)(2,1)S(1)}, u32[]{:S(2)}, u32[]{:S(2)}) collective-permute-start(bf16[4,8,2,32,128]{4,3,2,1,0:T(8,128)(2,1)S(1)} %copy-done.31), channel_id=1, source_target_pairs={{0,20},{1,21},{2,22},{3,23},{8,28},{9,29},{10,30},{11,31},{16,0},{... | collective-permute-start | bytes 1572872 | tf_op jit(solution)/shard_map/ppermute | solution.py:29
  163.8 6.6 %shard_map.38 = (f32[2,4,2,32,256]{4,3,2,1,0:T(8,128)}, f32[8,128]{1,0:T(8,128)S(1)}) custom-call(s32[5]{0:T(128)S(1)} %copy-done.9, bf16[4,8,2,32,128]{4,3,2,1,0:T(8,128)(2,1)S(1)} %copy-done.5, bf16[4,8,2,32,128]{4,3,2,1,0:T(8,128)(2,1)} %collective-permute-done.20.r_2_, bf16[4,8,2,32,128]{4,3,2,1,0:T(8,128)(2,1)} %collective-permute-done.21.r_3_, ...), custom_call_target="tpu_custom_call" | custom-call | flops 2147483648 | bytes 11534336 | tf_op jit(solution)/shard_map/pallas_call | solution.py:175
  170.4 2.7 %collective-permute-start.36 = (f32[2,4,2,32,256]{4,3,2,1,0:T(8,128)}, f32[2,4,2,32,256]{4,3,2,1,0:T(8,128)}, u32[]{:S(2)}, u32[]{:S(2)}) collective-permute-start(f32[2,4,2,32,256]{4,3,2,1,0:T(8,128)} %get-tuple-element.74), channel_id=1, source_target_pairs={{0,64},{1,65},{2,66},{3,67},{8,72},{9,73},{10,74},{11,75},{16,80},... | collective-permute-start | bytes 1572872 | tf_op jit(solution)/shard_map/ppermute | solution.py:29
  173.7 6.6 %shard_map.42 = (f32[2,4,2,32,256]{4,3,2,1,0:T(8,128)}, f32[8,128]{1,0:T(8,128)S(1)}) custom-call(s32[5]{0:T(128)S(1)} %copy-done.9, bf16[4,8,2,32,128]{4,3,2,1,0:T(8,128)(2,1)S(1)} %copy-done.6, bf16[4,8,2,32,128]{4,3,2,1,0:T(8,128)(2,1)} %collective-permute-done.32.r_2_, bf16[4,8,2,32,128]{4,3,2,1,0:T(8,128)(2,1)} %collective-permute-done.33.r_3_, ...), custom_call_target="tpu_custom_call" | custom-call | flops 2147483648 | bytes 11534336 | tf_op jit(solution)/shard_map/pallas_call | solution.py:175
  180.3 2.0 collective-permute-start.37
  182.3 3.3 %collective-permute-done.4.r_3_ = bf16[4,8,2,32,128]{4,3,2,1,0:T(8,128)(2,1)S(1)} collective-permute-done((bf16[4,8,2,32,128]{4,3,2,1,0:T(8,128)(2,1)S(1)}, bf16[4,8,2,32,128]{4,3,2,1,0:T(8,128)(2,1)S(1)}, u32[]{:S(2)}, u32[]{:S(2)}) %collective-permute-start.4) | collective-permute-done | bytes 524320 | tf_op jit(solution)/shard_map/ppermute | solution.py:29
  185.7 9.4 %collective-permute-done.5.r_4_ = bf16[4,8,2,32,128]{4,3,2,1,0:T(8,128)(2,1)S(1)} collective-permute-done((bf16[4,8,2,32,128]{4,3,2,1,0:T(8,128)(2,1)S(1)}, bf16[4,8,2,32,128]{4,3,2,1,0:T(8,128)(2,1)S(1)}, u32[]{:S(2)}, u32[]{:S(2)}) %collective-permute-start.5) | collective-permute-done | bytes 524320 | tf_op jit(solution)/shard_map/ppermute | solution.py:29
  195.1 6.1 %shard_map.43 = (f32[2,4,2,32,256]{4,3,2,1,0:T(8,128)S(1)}, f32[128,128]{1,0:T(8,128)}) custom-call(s32[5]{0:T(128)S(1)} %copy-done.9, bf16[4,8,2,32,128]{4,3,2,1,0:T(8,128)(2,1)S(1)} %copy-done.7, bf16[4,8,2,32,128]{4,3,2,1,0:T(8,128)(2,1)S(1)} %collective-permute-done.3.r_2_, bf16[4,8,2,32,128]{4,3,2,1,0:T(8,128)(2,1)S(1)} %collective-permute-done.4.r_3_, ...), custom_call_target="tpu_custom_call" | custom-call | flops 2147483648 | bytes 11534336 | tf_op jit(solution)/shard_map/pallas_call | solution.py:175
  202.0 5.3 %all-to-all-start.1 = ((f32[128,1,128]{2,1,0:T(1,128)}), f32[128,1,128]{2,1,0:T(1,128)S(1)}, u32[]{:S(2)}, u32[]{:S(2)}) async-start(f32[128,1,128]{2,1,0:T(1,128)} %bitcast.9), calls=%async_computation.1 | async-start | bytes 131072 | tf_op jit(solution)/shard_map/all_to_all | solution.py:288
  207.3 9.8 %all-to-all-done.1 = f32[128,1,128]{2,1,0:T(1,128)S(1)} async-done(((f32[128,1,128]{2,1,0:T(1,128)}), f32[128,1,128]{2,1,0:T(1,128)S(1)}, u32[]{:S(2)}, u32[]{:S(2)}) %all-to-all-start.1) | async-done | bytes 65568 | tf_op jit(solution)/shard_map/all_to_all | solution.py:288
  217.8 3.4 %shard_map.44 = (bf16[4,2,32,256]{3,2,1,0:T(8,128)(2,1)}, bf16[4,2,32,256]{3,2,1,0:T(8,128)(2,1)}, bf16[4,2,32,256]{3,2,1,0:T(8,128)(2,1)}, bf16[4,2,32,256]{3,2...) custom-call(s32[5]{0:T(128)} %stack.23.where.r_0_, ...), custom_call_target="tpu_custom_call" | custom-call | flops 4325376 | bytes 4325376 | tf_op jit(solution)/shard_map/pallas_call | solution.py:35
  222.0 1.4 collective-permute-start.40
  224.0 2.3 collective-permute-start.42
  226.9 2.1 collective-permute-start.44
  228.9 1.5 collective-permute-done.40.refs_3_
  230.6 2.4 collective-permute-done.43.refs_6_
  233.0 3.0 %collective-permute-done.44.refs_7_ = bf16[4,2,32,256]{3,2,1,0:T(8,128)(2,1)S(1)} collective-permute-done((bf16[4,2,32,256]{3,2,1,0:T(8,128)(2,1)}, bf16[4,2,32,256]{3,2,1,0:T(8,128)(2,1)S(1)}, u32[]{:S(2)}, u32[]{:S(2)}) %collective-permute-start.44) | collective-permute-done | bytes 131104 | tf_op jit(solution)/shard_map/ppermute | solution.py:29
  236.6 4.0 %shard_map.45 = bf16[32,32,2,256]{3,2,1,0:T(2,128)(2,1)} custom-call(s32[5]{0:T(128)} %stack.23.where.r_0_, bf16[4,2,32,256]{3,2,1,0:T(8,128)(2,1)} %get-tuple-element.77.refs_0_, bf16[4,2,32,256]{3,2,1,0:T(8,128)(2,1)} %copy-done.17, bf16[4,2,32,256]{3,2,1,0:T(8,128)(2,1)} %copy-done.18, bf16[4,2,32,256]{3,2,1,0:T(8,128)(2,1)} %copy-done.19, ...), custom_call_target="tpu_custom_call" | custom-call | flops 2097152 | bytes 2097152 | tf_op jit(solution)/shard_map/pallas_call | solution.py:35
  (113 shorter events, 12.5 us)
Async XLA Ops:
  4.0 8.6 %collective-permute-start.10 = (bf16[2,2,2,2,32,128]{5,4,3,2,1,0:T(8,128)(2,1)}, bf16[2,2,2,2,32,128]{5,4,3,2,1,0:T(8,128)(2,1)S(1)}, u32[]{:S(2)}, u32[]{:S(2)}) collective-permute-start(bf16[2,2,2,2,32,128]{5,4,3,2,1,0:T(8,128)(2,1)} %get-tuple-element.50), channel_id=1, source_target_pairs={{0,32},{1,33},{2,34},{3,35},{8,40},{9,41},{10,42},{11,43},{16,48},... | collective-permute-start | bytes 393224 | tf_op jit(solution)/shard_map/ppermute | solution.py:29
  6.5 9.2 %collective-permute-start.11 = (bf16[2,2,2,2,32,128]{5,4,3,2,1,0:T(8,128)(2,1)}, bf16[2,2,2,2,32,128]{5,4,3,2,1,0:T(8,128)(2,1)S(1)}, u32[]{:S(2)}, u32[]{:S(2)}) collective-permute-start(bf16[2,2,2,2,32,128]{5,4,3,2,1,0:T(8,128)(2,1)} %get-tuple-element.51), channel_id=1, source_target_pairs={{0,64},{1,65},{2,66},{3,67},{8,72},{9,73},{10,74},{11,75},{16,80},... | collective-permute-start | bytes 393224 | tf_op jit(solution)/shard_map/ppermute | solution.py:29
  9.8 7.1 %collective-permute-start.12 = (bf16[2,2,2,2,32,128]{5,4,3,2,1,0:T(8,128)(2,1)}, bf16[2,2,2,2,32,128]{5,4,3,2,1,0:T(8,128)(2,1)S(1)}, u32[]{:S(2)}, u32[]{:S(2)}) collective-permute-start(bf16[2,2,2,2,32,128]{5,4,3,2,1,0:T(8,128)(2,1)} %get-tuple-element.52), channel_id=1, source_target_pairs={{0,96},{1,97},{2,98},{3,99},{8,104},{9,105},{10,106},{11,107},{16,... | collective-permute-start | bytes 393224 | tf_op jit(solution)/shard_map/ppermute | solution.py:29
  10.5 6.4 %collective-permute-start.13 = (bf16[2,2,2,2,32,128]{5,4,3,2,1,0:T(8,128)(2,1)}, bf16[2,2,2,2,32,128]{5,4,3,2,1,0:T(8,128)(2,1)S(1)}, u32[]{:S(2)}, u32[]{:S(2)}) collective-permute-start(bf16[2,2,2,2,32,128]{5,4,3,2,1,0:T(8,128)(2,1)} %get-tuple-element.53), channel_id=1, source_target_pairs={{0,8},{1,9},{2,10},{3,11},{8,0},{9,1},{10,2},{11,3},{16,24},{17,25... | collective-permute-start | bytes 393224 | tf_op jit(solution)/shard_map/ppermute | solution.py:29
  12.1 10.3 %collective-permute-start.14 = (bf16[2,2,2,2,32,128]{5,4,3,2,1,0:T(8,128)(2,1)}, bf16[2,2,2,2,32,128]{5,4,3,2,1,0:T(8,128)(2,1)S(1)}, u32[]{:S(2)}, u32[]{:S(2)}) collective-permute-start(bf16[2,2,2,2,32,128]{5,4,3,2,1,0:T(8,128)(2,1)} %get-tuple-element.54), channel_id=1, source_target_pairs={{0,40},{1,41},{2,42},{3,43},{8,32},{9,33},{10,34},{11,35},{16,56},... | collective-permute-start | bytes 393224 | tf_op jit(solution)/shard_map/ppermute | solution.py:29
  12.7 9.7 %copy-start.24 = (bf16[2,2,2,2,32,128]{5,4,3,2,1,0:T(8,128)(2,1)}, bf16[2,2,2,2,32,128]{5,4,3,2,1,0:T(8,128)(2,1)S(1)}, u32[]{:S(2)}) copy-start(bf16[2,2,2,2,32,128]{5,4,3,2,1,0:T(8,128)(2,1)S(1)} %collective-permute-done.10.refs_1_) | copy-start | bytes 393220
  12.7 9.7 %collective-permute-start.15 = (bf16[2,2,2,2,32,128]{5,4,3,2,1,0:T(8,128)(2,1)}, bf16[2,2,2,2,32,128]{5,4,3,2,1,0:T(8,128)(2,1)S(1)}, u32[]{:S(2)}, u32[]{:S(2)}) collective-permute-start(bf16[2,2,2,2,32,128]{5,4,3,2,1,0:T(8,128)(2,1)} %get-tuple-element.55), channel_id=1, source_target_pairs={{0,72},{1,73},{2,74},{3,75},{8,64},{9,65},{10,66},{11,67},{16,88},... | collective-permute-start | bytes 393224 | tf_op jit(solution)/shard_map/ppermute | solution.py:29
  15.7 6.7 %copy-start.25 = (bf16[2,2,2,2,32,128]{5,4,3,2,1,0:T(8,128)(2,1)}, bf16[2,2,2,2,32,128]{5,4,3,2,1,0:T(8,128)(2,1)S(1)}, u32[]{:S(2)}) copy-start(bf16[2,2,2,2,32,128]{5,4,3,2,1,0:T(8,128)(2,1)S(1)} %collective-permute-done.11.refs_2_) | copy-start | bytes 393220
  15.7 6.6 %collective-permute-start.16 = (bf16[2,2,2,2,32,128]{5,4,3,2,1,0:T(8,128)(2,1)}, bf16[2,2,2,2,32,128]{5,4,3,2,1,0:T(8,128)(2,1)S(1)}, u32[]{:S(2)}, u32[]{:S(2)}) collective-permute-start(bf16[2,2,2,2,32,128]{5,4,3,2,1,0:T(8,128)(2,1)} %get-tuple-element.56), channel_id=1, source_target_pairs={{0,104},{1,105},{2,106},{3,107},{8,96},{9,97},{10,98},{11,99},{16,... | collective-permute-start | bytes 393224 | tf_op jit(solution)/shard_map/ppermute | solution.py:29
  16.9 5.5 %copy-start.26 = (bf16[2,2,2,2,32,128]{5,4,3,2,1,0:T(8,128)(2,1)}, bf16[2,2,2,2,32,128]{5,4,3,2,1,0:T(8,128)(2,1)S(1)}, u32[]{:S(2)}) copy-start(bf16[2,2,2,2,32,128]{5,4,3,2,1,0:T(8,128)(2,1)S(1)} %collective-permute-done.12.refs_3_) | copy-start | bytes 393220
  16.9 5.5 %copy-start.27 = (bf16[2,2,2,2,32,128]{5,4,3,2,1,0:T(8,128)(2,1)}, bf16[2,2,2,2,32,128]{5,4,3,2,1,0:T(8,128)(2,1)S(1)}, u32[]{:S(2)}) copy-start(bf16[2,2,2,2,32,128]{5,4,3,2,1,0:T(8,128)(2,1)S(1)} %collective-permute-done.13.refs_4_) | copy-start | bytes 393220
  26.1 8.8 %collective-permute-start.23 = (bf16[2,8,2,32,128]{4,3,2,1,0:T(8,128)(2,1)}, bf16[2,8,2,32,128]{4,3,2,1,0:T(8,128)(2,1)S(1)}, u32[]{:S(2)}, u32[]{:S(2)}) collective-permute-start(bf16[2,8,2,32,128]{4,3,2,1,0:T(8,128)(2,1)} %get-tuple-element.62.refs_0_), channel_id=1, source_target_pairs={{0,2},{1,3},{2,0},{3,1},{8,10},{9,11},{10,8},{11,9},{16,18},{17,19... | collective-permute-start | bytes 786440 | tf_op jit(solution)/shard_map/ppermute | solution.py:29
  29.0 13.7 %collective-permute-start.24 = (bf16[2,8,2,32,128]{4,3,2,1,0:T(8,128)(2,1)}, bf16[2,8,2,32,128]{4,3,2,1,0:T(8,128)(2,1)S(1)}, u32[]{:S(2)}, u32[]{:S(2)}) collective-permute-start(bf16[2,8,2,32,128]{4,3,2,1,0:T(8,128)(2,1)} %get-tuple-element.63), channel_id=1, source_target_pairs={{0,1},{1,2},{2,3},{3,0},{8,9},{9,10},{10,11},{11,8},{16,17},{17,18... | collective-permute-start | bytes 786440 | tf_op jit(solution)/shard_map/ppermute | solution.py:29
  29.4 13.3 %collective-permute-start.25 = (bf16[2,8,2,32,128]{4,3,2,1,0:T(8,128)(2,1)}, bf16[2,8,2,32,128]{4,3,2,1,0:T(8,128)(2,1)S(1)}, u32[]{:S(2)}, u32[]{:S(2)}) collective-permute-start(bf16[2,8,2,32,128]{4,3,2,1,0:T(8,128)(2,1)} %get-tuple-element.63), channel_id=1, source_target_pairs={{0,3},{1,0},{2,1},{3,2},{8,11},{9,8},{10,9},{11,10},{16,19},{17,16... | collective-permute-start | bytes 786440 | tf_op jit(solution)/shard_map/ppermute | solution.py:29
  31.7 21.1 %collective-permute-start.17 = (bf16[2,8,2,32,128]{4,3,2,1,0:T(8,128)(2,1)}, bf16[2,8,2,32,128]{4,3,2,1,0:T(8,128)(2,1)S(1)}, u32[]{:S(2)}, u32[]{:S(2)}) collective-permute-start(bf16[2,8,2,32,128]{4,3,2,1,0:T(8,128)(2,1)} %get-tuple-element.57.refs_0_), channel_id=1, source_target_pairs={{0,2},{1,3},{2,0},{3,1},{8,10},{9,11},{10,8},{11,9},{16,18},{17,19... | collective-permute-start | bytes 786440 | tf_op jit(solution)/shard_map/ppermute | solution.py:29
  35.0 7.8 %copy-start.14 = (bf16[2,8,2,32,128]{4,3,2,1,0:T(8,128)(2,1)}, bf16[2,8,2,32,128]{4,3,2,1,0:T(8,128)(2,1)S(1)}, u32[]{:S(2)}) copy-start(bf16[2,8,2,32,128]{4,3,2,1,0:T(8,128)(2,1)S(1)} %collective-permute-done.23.refs_1_) | copy-start | bytes 786436
  47.1 26.4 %collective-permute-start.26 = (bf16[4,8,2,32,128]{4,3,2,1,0:T(8,128)(2,1)}, bf16[4,8,2,32,128]{4,3,2,1,0:T(8,128)(2,1)S(1)}, u32[]{:S(2)}, u32[]{:S(2)}) collective-permute-start(bf16[4,8,2,32,128]{4,3,2,1,0:T(8,128)(2,1)} %get-tuple-element.64.r_1_), channel_id=1, source_target_pairs={{0,4},{1,5},{2,6},{3,7},{8,12},{9,13},{10,14},{11,15},{16,20},{17,... | collective-permute-start | bytes 1572872 | tf_op jit(solution)/shard_map/ppermute | solution.py:29
  49.9 17.6 %collective-permute-start.18 = (bf16[2,8,2,32,128]{4,3,2,1,0:T(8,128)(2,1)}, bf16[2,8,2,32,128]{4,3,2,1,0:T(8,128)(2,1)}, u32[]{:S(2)}, u32[]{:S(2)}) collective-permute-start(bf16[2,8,2,32,128]{4,3,2,1,0:T(8,128)(2,1)} %get-tuple-element.58), channel_id=1, source_target_pairs={{0,1},{1,2},{2,3},{3,0},{8,9},{9,10},{10,11},{11,8},{16,17},{17,18... | collective-permute-start | bytes 786440 | tf_op jit(solution)/shard_map/ppermute | solution.py:29
  50.4 20.0 %collective-permute-start.19 = (bf16[2,8,2,32,128]{4,3,2,1,0:T(8,128)(2,1)}, bf16[2,8,2,32,128]{4,3,2,1,0:T(8,128)(2,1)}, u32[]{:S(2)}, u32[]{:S(2)}) collective-permute-start(bf16[2,8,2,32,128]{4,3,2,1,0:T(8,128)(2,1)} %get-tuple-element.58), channel_id=1, source_target_pairs={{0,3},{1,0},{2,1},{3,2},{8,11},{9,8},{10,9},{11,10},{16,19},{17,16... | collective-permute-start | bytes 786440 | tf_op jit(solution)/shard_map/ppermute | solution.py:29
  52.5 23.7 %collective-permute-start.27 = (bf16[4,8,2,32,128]{4,3,2,1,0:T(8,128)(2,1)}, bf16[4,8,2,32,128]{4,3,2,1,0:T(8,128)(2,1)S(1)}, u32[]{:S(2)}, u32[]{:S(2)}) collective-permute-start(bf16[4,8,2,32,128]{4,3,2,1,0:T(8,128)(2,1)} %get-tuple-element.65), channel_id=1, source_target_pairs={{0,16},{1,17},{2,18},{3,19},{8,24},{9,25},{10,26},{11,27},{16,4},{... | collective-permute-start | bytes 1572872 | tf_op jit(solution)/shard_map/ppermute | solution.py:29
  52.9 17.6 %copy-start.11 = (bf16[2,8,2,32,128]{4,3,2,1,0:T(8,128)(2,1)}, bf16[2,8,2,32,128]{4,3,2,1,0:T(8,128)(2,1)S(1)}, u32[]{:S(2)}) copy-start(bf16[2,8,2,32,128]{4,3,2,1,0:T(8,128)(2,1)S(1)} %collective-permute-done.17.refs_1_) | copy-start | bytes 786436
  52.9 24.5 %collective-permute-start.28 = (bf16[4,8,2,32,128]{4,3,2,1,0:T(8,128)(2,1)}, bf16[4,8,2,32,128]{4,3,2,1,0:T(8,128)(2,1)}, u32[]{:S(2)}, u32[]{:S(2)}) collective-permute-start(bf16[4,8,2,32,128]{4,3,2,1,0:T(8,128)(2,1)} %get-tuple-element.65), channel_id=1, source_target_pairs={{0,20},{1,21},{2,22},{3,23},{8,28},{9,29},{10,30},{11,31},{16,0},{... | collective-permute-start | bytes 1572872 | tf_op jit(solution)/shard_map/ppermute | solution.py:29
  58.6 30.4 %all-to-all-start = ((bf16[8,2,2,2,2,32,128]{6,5,4,3,2,1,0:T(8,128)(2,1)}), bf16[8,2,2,2,2,32,128]{6,5,4,3,2,1,0:T(8,128)(2,1)}, u32[]{:S(2)}, u32[]{:S(2)}) async-start(bf16[8,2,2,2,2,32,128]{6,5,4,3,2,1,0:T(8,128)(2,1)} %shard_map.28), calls=%async_computation | async-start | bytes 2097152 | tf_op jit(solution)/shard_map/all_to_all | solution.py:257
  67.5 36.6 %collective-permute-start.6 = (bf16[256,2048]{1,0:T(8,128)(2,1)}, bf16[256,2048]{1,0:T(8,128)(2,1)S(1)}, u32[]{:S(2)}, u32[]{:S(2)}) collective-permute-start(bf16[256,2048]{1,0:T(8,128)(2,1)} %shard_map.31), channel_id=1, source_target_pairs={{0,3},{1,0},{2,1},{3,2},{8,9},{9,10},{10,11},{11,8},{16,19},{17,16... | collective-permute-start | bytes 3145736 | tf_op jit(solution)/shard_map/ppermute | solution.py:29
  70.5 33.6 %collective-permute-start.7 = (bf16[256,2048]{1,0:T(8,128)(2,1)}, bf16[256,2048]{1,0:T(8,128)(2,1)S(1)}, u32[]{:S(2)}, u32[]{:S(2)}) collective-permute-start(bf16[256,2048]{1,0:T(8,128)(2,1)} %shard_map.32), channel_id=1, source_target_pairs={{0,3},{1,0},{2,1},{3,2},{8,9},{9,10},{10,11},{11,8},{16,19},{17,16... | collective-permute-start | bytes 3145736 | tf_op jit(solution)/shard_map/ppermute | solution.py:29
  73.5 14.4 %collective-permute-start.20 = (bf16[4,8,2,32,128]{4,3,2,1,0:T(8,128)(2,1)}, bf16[4,8,2,32,128]{4,3,2,1,0:T(8,128)(2,1)}, u32[]{:S(2)}, u32[]{:S(2)}) collective-permute-start(bf16[4,8,2,32,128]{4,3,2,1,0:T(8,128)(2,1)} %get-tuple-element.59.r_1_), channel_id=1, source_target_pairs={{0,4},{1,5},{2,6},{3,7},{8,12},{9,13},{10,14},{11,15},{16,20},{17,... | collective-permute-start | bytes 1572872 | tf_op jit(solution)/shard_map/ppermute | solution.py:29
  76.2 69.6 %copy-start.9 = (s32[5]{0:T(128)S(1)}, s32[5]{0:T(128)}, u32[]{:S(2)}) copy-start(s32[5]{0:T(128)} %stack.23.where.r_0_) | copy-start | bytes 64
  77.0 23.4 %collective-permute-start.21 = (bf16[4,8,2,32,128]{4,3,2,1,0:T(8,128)(2,1)}, bf16[4,8,2,32,128]{4,3,2,1,0:T(8,128)(2,1)}, u32[]{:S(2)}, u32[]{:S(2)}) collective-permute-start(bf16[4,8,2,32,128]{4,3,2,1,0:T(8,128)(2,1)} %get-tuple-element.60), channel_id=1, source_target_pairs={{0,16},{1,17},{2,18},{3,19},{8,24},{9,25},{10,26},{11,27},{16,4},{... | collective-permute-start | bytes 1572872 | tf_op jit(solution)/shard_map/ppermute | solution.py:29
  77.3 58.7 %collective-permute-start.8 = (bf16[256,2048]{1,0:T(8,128)(2,1)}, bf16[256,2048]{1,0:T(8,128)(2,1)S(1)}, u32[]{:S(2)}, u32[]{:S(2)}) collective-permute-start(bf16[256,2048]{1,0:T(8,128)(2,1)} %shard_map.33), channel_id=1, source_target_pairs={{0,3},{1,0},{2,1},{3,2},{8,9},{9,10},{10,11},{11,8},{16,19},{17,16... | collective-permute-start | bytes 3145736 | tf_op jit(solution)/shard_map/ppermute | solution.py:29
  87.8 58.0 %collective-permute-start.9 = (bf16[256,2048]{1,0:T(8,128)(2,1)}, bf16[256,2048]{1,0:T(8,128)(2,1)}, u32[]{:S(2)}, u32[]{:S(2)}) collective-permute-start(bf16[256,2048]{1,0:T(8,128)(2,1)} %shard_map.34), channel_id=1, source_target_pairs={{0,3},{1,0},{2,1},{3,2},{8,9},{9,10},{10,11},{11,8},{16,19},{17,16... | collective-permute-start | bytes 3145736 | tf_op jit(solution)/shard_map/ppermute | solution.py:29
  100.4 26.5 %collective-permute-start.29 = (bf16[2,8,2,32,128]{4,3,2,1,0:T(8,128)(2,1)}, bf16[2,8,2,32,128]{4,3,2,1,0:T(8,128)(2,1)S(1)}, u32[]{:S(2)}, u32[]{:S(2)}) collective-permute-start(bf16[2,8,2,32,128]{4,3,2,1,0:T(8,128)(2,1)} %get-tuple-element.67.refs_0_), channel_id=1, source_target_pairs={{0,2},{1,3},{2,0},{3,1},{8,10},{9,11},{10,8},{11,9},{16,18},{17,19... | collective-permute-start | bytes 786440 | tf_op jit(solution)/shard_map/ppermute | solution.py:29
  104.1 26.3 %collective-permute-start.30 = (bf16[2,8,2,32,128]{4,3,2,1,0:T(8,128)(2,1)}, bf16[2,8,2,32,128]{4,3,2,1,0:T(8,128)(2,1)}, u32[]{:S(2)}, u32[]{:S(2)}) collective-permute-start(bf16[2,8,2,32,128]{4,3,2,1,0:T(8,128)(2,1)} %get-tuple-element.68), channel_id=1, source_target_pairs={{0,1},{1,2},{2,3},{3,0},{8,9},{9,10},{10,11},{11,8},{16,17},{17,18... | collective-permute-start | bytes 786440 | tf_op jit(solution)/shard_map/ppermute | solution.py:29
  104.1 26.3 %collective-permute-start.31 = (bf16[2,8,2,32,128]{4,3,2,1,0:T(8,128)(2,1)}, bf16[2,8,2,32,128]{4,3,2,1,0:T(8,128)(2,1)}, u32[]{:S(2)}, u32[]{:S(2)}) collective-permute-start(bf16[2,8,2,32,128]{4,3,2,1,0:T(8,128)(2,1)} %get-tuple-element.68), channel_id=1, source_target_pairs={{0,3},{1,0},{2,1},{3,2},{8,11},{9,8},{10,9},{11,10},{16,19},{17,16... | collective-permute-start | bytes 786440 | tf_op jit(solution)/shard_map/ppermute | solution.py:29
  127.6 8.4 %collective-permute-start = (bf16[2,8,2,32,128]{4,3,2,1,0:T(8,128)(2,1)}, bf16[2,8,2,32,128]{4,3,2,1,0:T(8,128)(2,1)S(1)}, u32[]{:S(2)}, u32[]{:S(2)}) collective-permute-start(bf16[2,8,2,32,128]{4,3,2,1,0:T(8,128)(2,1)} %get-tuple-element.45.refs_0_), channel_id=1, source_target_pairs={{0,2},{1,3},{2,0},{3,1},{8,10},{9,11},{10,8},{11,9},{16,18},{17,19... | collective-permute-start | bytes 786440 | tf_op jit(solution)/shard_map/ppermute | solution.py:29
  130.4 9.9 %collective-permute-start.1 = (bf16[2,8,2,32,128]{4,3,2,1,0:T(8,128)(2,1)}, bf16[2,8,2,32,128]{4,3,2,1,0:T(8,128)(2,1)}, u32[]{:S(2)}, u32[]{:S(2)}) collective-permute-start(bf16[2,8,2,32,128]{4,3,2,1,0:T(8,128)(2,1)} %get-tuple-element.46), channel_id=1, source_target_pairs={{0,1},{1,2},{2,3},{3,0},{8,9},{9,10},{10,11},{11,8},{16,17},{17,18... | collective-permute-start | bytes 786440 | tf_op jit(solution)/shard_map/ppermute | solution.py:29
  130.4 11.1 %collective-permute-start.2 = (bf16[2,8,2,32,128]{4,3,2,1,0:T(8,128)(2,1)}, bf16[2,8,2,32,128]{4,3,2,1,0:T(8,128)(2,1)}, u32[]{:S(2)}, u32[]{:S(2)}) collective-permute-start(bf16[2,8,2,32,128]{4,3,2,1,0:T(8,128)(2,1)} %get-tuple-element.46), channel_id=1, source_target_pairs={{0,3},{1,0},{2,1},{3,2},{8,11},{9,8},{10,9},{11,10},{16,19},{17,16... | collective-permute-start | bytes 786440 | tf_op jit(solution)/shard_map/ppermute | solution.py:29
  136.0 19.2 %collective-permute-start.22 = (bf16[4,8,2,32,128]{4,3,2,1,0:T(8,128)(2,1)}, bf16[4,8,2,32,128]{4,3,2,1,0:T(8,128)(2,1)}, u32[]{:S(2)}, u32[]{:S(2)}) collective-permute-start(bf16[4,8,2,32,128]{4,3,2,1,0:T(8,128)(2,1)} %get-tuple-element.60), channel_id=1, source_target_pairs={{0,20},{1,21},{2,22},{3,23},{8,28},{9,29},{10,30},{11,31},{16,0},{... | collective-permute-start | bytes 1572872 | tf_op jit(solution)/shard_map/ppermute | solution.py:29
  136.0 6.9 %copy-start.12 = (bf16[2,8,2,32,128]{4,3,2,1,0:T(8,128)(2,1)}, bf16[2,8,2,32,128]{4,3,2,1,0:T(8,128)(2,1)S(1)}, u32[]{:S(2)}) copy-start(bf16[2,8,2,32,128]{4,3,2,1,0:T(8,128)(2,1)S(1)} %collective-permute-done.refs_1_) | copy-start | bytes 786436
  136.0 24.4 %collective-permute-start.32 = (bf16[4,8,2,32,128]{4,3,2,1,0:T(8,128)(2,1)}, bf16[4,8,2,32,128]{4,3,2,1,0:T(8,128)(2,1)}, u32[]{:S(2)}, u32[]{:S(2)}) collective-permute-start(bf16[4,8,2,32,128]{4,3,2,1,0:T(8,128)(2,1)} %get-tuple-element.69.r_1_), channel_id=1, source_target_pairs={{0,4},{1,5},{2,6},{3,7},{8,12},{9,13},{10,14},{11,15},{16,20},{17,... | collective-permute-start | bytes 1572872 | tf_op jit(solution)/shard_map/ppermute | solution.py:29
  140.2 30.1 %collective-permute-start.33 = (bf16[4,8,2,32,128]{4,3,2,1,0:T(8,128)(2,1)}, bf16[4,8,2,32,128]{4,3,2,1,0:T(8,128)(2,1)}, u32[]{:S(2)}, u32[]{:S(2)}) collective-permute-start(bf16[4,8,2,32,128]{4,3,2,1,0:T(8,128)(2,1)} %get-tuple-element.70), channel_id=1, source_target_pairs={{0,16},{1,17},{2,18},{3,19},{8,24},{9,25},{10,26},{11,27},{16,4},{... | collective-permute-start | bytes 1572872 | tf_op jit(solution)/shard_map/ppermute | solution.py:29
  141.5 31.6 %collective-permute-start.34 = (bf16[4,8,2,32,128]{4,3,2,1,0:T(8,128)(2,1)}, bf16[4,8,2,32,128]{4,3,2,1,0:T(8,128)(2,1)}, u32[]{:S(2)}, u32[]{:S(2)}) collective-permute-start(bf16[4,8,2,32,128]{4,3,2,1,0:T(8,128)(2,1)} %get-tuple-element.70), channel_id=1, source_target_pairs={{0,20},{1,21},{2,22},{3,23},{8,28},{9,29},{10,30},{11,31},{16,0},{... | collective-permute-start | bytes 1572872 | tf_op jit(solution)/shard_map/ppermute | solution.py:29
  145.8 34.5 %collective-permute-start.3 = (bf16[4,8,2,32,128]{4,3,2,1,0:T(8,128)(2,1)}, bf16[4,8,2,32,128]{4,3,2,1,0:T(8,128)(2,1)S(1)}, u32[]{:S(2)}, u32[]{:S(2)}) collective-permute-start(bf16[4,8,2,32,128]{4,3,2,1,0:T(8,128)(2,1)} %get-tuple-element.47.r_1_), channel_id=1, source_target_pairs={{0,4},{1,5},{2,6},{3,7},{8,12},{9,13},{10,14},{11,15},{16,20},{17,... | collective-permute-start | bytes 1572872 | tf_op jit(solution)/shard_map/ppermute | solution.py:29
  149.0 6.3 %copy-start.31 = (bf16[4,8,2,32,128]{4,3,2,1,0:T(8,128)(2,1)S(1)}, bf16[4,8,2,32,128]{4,3,2,1,0:T(8,128)(2,1)}, u32[]{:S(2)}) copy-start(bf16[4,8,2,32,128]{4,3,2,1,0:T(8,128)(2,1)} %get-tuple-element.48) | copy-start | bytes 1572868
  149.0 14.8 %copy-start.5 = (bf16[4,8,2,32,128]{4,3,2,1,0:T(8,128)(2,1)S(1)}, bf16[4,8,2,32,128]{4,3,2,1,0:T(8,128)(2,1)}, u32[]{:S(2)}) copy-start(bf16[4,8,2,32,128]{4,3,2,1,0:T(8,128)(2,1)} %get-tuple-element.59.r_1_) | copy-start | bytes 1572868
  155.2 18.5 %copy-start.6 = (bf16[4,8,2,32,128]{4,3,2,1,0:T(8,128)(2,1)S(1)}, bf16[4,8,2,32,128]{4,3,2,1,0:T(8,128)(2,1)}, u32[]{:S(2)}) copy-start(bf16[4,8,2,32,128]{4,3,2,1,0:T(8,128)(2,1)} %get-tuple-element.69.r_1_) | copy-start | bytes 1572868
  155.2 30.4 %collective-permute-start.4 = (bf16[4,8,2,32,128]{4,3,2,1,0:T(8,128)(2,1)S(1)}, bf16[4,8,2,32,128]{4,3,2,1,0:T(8,128)(2,1)S(1)}, u32[]{:S(2)}, u32[]{:S(2)}) collective-permute-start(bf16[4,8,2,32,128]{4,3,2,1,0:T(8,128)(2,1)S(1)} %copy-done.31), channel_id=1, source_target_pairs={{0,16},{1,17},{2,18},{3,19},{8,24},{9,25},{10,26},{11,27},{16,4},{... | collective-permute-start | bytes 1572872 | tf_op jit(solution)/shard_map/ppermute | solution.py:29
  160.4 34.7 %collective-permute-start.5 = (bf16[4,8,2,32,128]{4,3,2,1,0:T(8,128)(2,1)S(1)}, bf16[4,8,2,32,128]{4,3,2,1,0:T(8,128)(2,1)S(1)}, u32[]{:S(2)}, u32[]{:S(2)}) collective-permute-start(bf16[4,8,2,32,128]{4,3,2,1,0:T(8,128)(2,1)S(1)} %copy-done.31), channel_id=1, source_target_pairs={{0,20},{1,21},{2,22},{3,23},{8,28},{9,29},{10,30},{11,31},{16,0},{... | collective-permute-start | bytes 1572872 | tf_op jit(solution)/shard_map/ppermute | solution.py:29
  170.3 24.8 %copy-start.7 = (bf16[4,8,2,32,128]{4,3,2,1,0:T(8,128)(2,1)S(1)}, bf16[4,8,2,32,128]{4,3,2,1,0:T(8,128)(2,1)}, u32[]{:S(2)}) copy-start(bf16[4,8,2,32,128]{4,3,2,1,0:T(8,128)(2,1)} %get-tuple-element.47.r_1_) | copy-start | bytes 1572868
  170.4 37.0 %collective-permute-start.36 = (f32[2,4,2,32,256]{4,3,2,1,0:T(8,128)}, f32[2,4,2,32,256]{4,3,2,1,0:T(8,128)}, u32[]{:S(2)}, u32[]{:S(2)}) collective-permute-start(f32[2,4,2,32,256]{4,3,2,1,0:T(8,128)} %get-tuple-element.74), channel_id=1, source_target_pairs={{0,64},{1,65},{2,66},{3,67},{8,72},{9,73},{10,74},{11,75},{16,80},... | collective-permute-start | bytes 1572872 | tf_op jit(solution)/shard_map/ppermute | solution.py:29
  173.1 34.3 %collective-permute-start.35 = (f32[2,4,2,32,256]{4,3,2,1,0:T(8,128)}, f32[2,4,2,32,256]{4,3,2,1,0:T(8,128)}, u32[]{:S(2)}, u32[]{:S(2)}) collective-permute-start(f32[2,4,2,32,256]{4,3,2,1,0:T(8,128)} %get-tuple-element.73), channel_id=1, source_target_pairs={{0,32},{1,33},{2,34},{3,35},{8,40},{9,41},{10,42},{11,43},{16,48},... | collective-permute-start | bytes 1572872 | tf_op jit(solution)/shard_map/ppermute | solution.py:29
  180.3 36.8 %collective-permute-start.37 = (f32[2,4,2,32,256]{4,3,2,1,0:T(8,128)}, f32[2,4,2,32,256]{4,3,2,1,0:T(8,128)}, u32[]{:S(2)}, u32[]{:S(2)}) collective-permute-start(f32[2,4,2,32,256]{4,3,2,1,0:T(8,128)} %get-tuple-element.75), channel_id=1, source_target_pairs={{0,96},{1,97},{2,98},{3,99},{8,104},{9,105},{10,106},{11,107},{16,... | collective-permute-start | bytes 1572872 | tf_op jit(solution)/shard_map/ppermute | solution.py:29
  202.0 15.2 %all-to-all-start.1 = ((f32[128,1,128]{2,1,0:T(1,128)}), f32[128,1,128]{2,1,0:T(1,128)S(1)}, u32[]{:S(2)}, u32[]{:S(2)}) async-start(f32[128,1,128]{2,1,0:T(1,128)} %bitcast.9), calls=%async_computation.1 | async-start | bytes 131072 | tf_op jit(solution)/shard_map/all_to_all | solution.py:288
  221.2 5.2 %collective-permute-start.38 = (bf16[4,2,32,256]{3,2,1,0:T(8,128)(2,1)}, bf16[4,2,32,256]{3,2,1,0:T(8,128)(2,1)S(1)}, u32[]{:S(2)}, u32[]{:S(2)}) collective-permute-start(bf16[4,2,32,256]{3,2,1,0:T(8,128)(2,1)} %get-tuple-element.78), channel_id=1, source_target_pairs={{0,8},{1,9},{2,10},{3,11},{8,0},{9,1},{10,2},{11,3},{16,24},{17,25... | collective-permute-start | bytes 393224 | tf_op jit(solution)/shard_map/ppermute | solution.py:29
  221.6 5.2 %collective-permute-start.39 = (bf16[4,2,32,256]{3,2,1,0:T(8,128)(2,1)}, bf16[4,2,32,256]{3,2,1,0:T(8,128)(2,1)S(1)}, u32[]{:S(2)}, u32[]{:S(2)}) collective-permute-start(bf16[4,2,32,256]{3,2,1,0:T(8,128)(2,1)} %get-tuple-element.79), channel_id=1, source_target_pairs={{0,16},{1,17},{2,18},{3,19},{8,24},{9,25},{10,26},{11,27},{16,0},{... | collective-permute-start | bytes 393224 | tf_op jit(solution)/shard_map/ppermute | solution.py:29
  222.0 8.4 %collective-permute-start.40 = (bf16[4,2,32,256]{3,2,1,0:T(8,128)(2,1)}, bf16[4,2,32,256]{3,2,1,0:T(8,128)(2,1)S(1)}, u32[]{:S(2)}, u32[]{:S(2)}) collective-permute-start(bf16[4,2,32,256]{3,2,1,0:T(8,128)(2,1)} %get-tuple-element.80), channel_id=1, source_target_pairs={{0,24},{1,25},{2,26},{3,27},{8,16},{9,17},{10,18},{11,19},{16,8},{... | collective-permute-start | bytes 393224 | tf_op jit(solution)/shard_map/ppermute | solution.py:29
  223.3 7.1 %collective-permute-start.41 = (bf16[4,2,32,256]{3,2,1,0:T(8,128)(2,1)}, bf16[4,2,32,256]{3,2,1,0:T(8,128)(2,1)S(1)}, u32[]{:S(2)}, u32[]{:S(2)}) collective-permute-start(bf16[4,2,32,256]{3,2,1,0:T(8,128)(2,1)} %get-tuple-element.81), channel_id=1, source_target_pairs={{0,1},{1,2},{2,3},{3,0},{8,11},{9,8},{10,9},{11,10},{16,17},{17,18... | collective-permute-start | bytes 393224 | tf_op jit(solution)/shard_map/ppermute | solution.py:29
  224.0 6.6 %collective-permute-start.42 = (bf16[4,2,32,256]{3,2,1,0:T(8,128)(2,1)}, bf16[4,2,32,256]{3,2,1,0:T(8,128)(2,1)S(1)}, u32[]{:S(2)}, u32[]{:S(2)}) collective-permute-start(bf16[4,2,32,256]{3,2,1,0:T(8,128)(2,1)} %get-tuple-element.82), channel_id=1, source_target_pairs={{0,9},{1,10},{2,11},{3,8},{8,3},{9,0},{10,1},{11,2},{16,25},{17,26... | collective-permute-start | bytes 393224 | tf_op jit(solution)/shard_map/ppermute | solution.py:29
  226.4 9.6 %copy-start.17 = (bf16[4,2,32,256]{3,2,1,0:T(8,128)(2,1)}, bf16[4,2,32,256]{3,2,1,0:T(8,128)(2,1)S(1)}, u32[]{:S(2)}) copy-start(bf16[4,2,32,256]{3,2,1,0:T(8,128)(2,1)S(1)} %collective-permute-done.38.refs_1_) | copy-start | bytes 393220
  226.4 6.6 %collective-permute-start.43 = (bf16[4,2,32,256]{3,2,1,0:T(8,128)(2,1)}, bf16[4,2,32,256]{3,2,1,0:T(8,128)(2,1)S(1)}, u32[]{:S(2)}, u32[]{:S(2)}) collective-permute-start(bf16[4,2,32,256]{3,2,1,0:T(8,128)(2,1)} %get-tuple-element.83), channel_id=1, source_target_pairs={{0,17},{1,18},{2,19},{3,16},{8,27},{9,24},{10,25},{11,26},{16,1},{... | collective-permute-start | bytes 393224 | tf_op jit(solution)/shard_map/ppermute | solution.py:29
  226.9 9.1 %copy-start.18 = (bf16[4,2,32,256]{3,2,1,0:T(8,128)(2,1)}, bf16[4,2,32,256]{3,2,1,0:T(8,128)(2,1)S(1)}, u32[]{:S(2)}) copy-start(bf16[4,2,32,256]{3,2,1,0:T(8,128)(2,1)S(1)} %collective-permute-done.39.refs_2_) | copy-start | bytes 393220
  226.9 9.1 %collective-permute-start.44 = (bf16[4,2,32,256]{3,2,1,0:T(8,128)(2,1)}, bf16[4,2,32,256]{3,2,1,0:T(8,128)(2,1)S(1)}, u32[]{:S(2)}, u32[]{:S(2)}) collective-permute-start(bf16[4,2,32,256]{3,2,1,0:T(8,128)(2,1)} %get-tuple-element.84), channel_id=1, source_target_pairs={{0,25},{1,26},{2,27},{3,24},{8,19},{9,16},{10,17},{11,18},{16,9},{... | collective-permute-start | bytes 393224 | tf_op jit(solution)/shard_map/ppermute | solution.py:29
  230.4 5.5 %copy-start.19 = (bf16[4,2,32,256]{3,2,1,0:T(8,128)(2,1)}, bf16[4,2,32,256]{3,2,1,0:T(8,128)(2,1)S(1)}, u32[]{:S(2)}) copy-start(bf16[4,2,32,256]{3,2,1,0:T(8,128)(2,1)S(1)} %collective-permute-done.40.refs_3_) | copy-start | bytes 393220
  230.4 5.5 %copy-start.20 = (bf16[4,2,32,256]{3,2,1,0:T(8,128)(2,1)}, bf16[4,2,32,256]{3,2,1,0:T(8,128)(2,1)S(1)}, u32[]{:S(2)}) copy-start(bf16[4,2,32,256]{3,2,1,0:T(8,128)(2,1)S(1)} %collective-permute-done.41.refs_4_) | copy-start | bytes 393220
  230.6 5.4 %copy-start.21 = (bf16[4,2,32,256]{3,2,1,0:T(8,128)(2,1)}, bf16[4,2,32,256]{3,2,1,0:T(8,128)(2,1)S(1)}, u32[]{:S(2)}) copy-start(bf16[4,2,32,256]{3,2,1,0:T(8,128)(2,1)S(1)} %collective-permute-done.42.refs_5_) | copy-start | bytes 393220
  (15 other events, 17.1 us)
